TPU v7x, 256 devices: a whole 4x4x8 slice. The times are simulated.
256 devices in a mesh: rep: 8 (over z), ep: 4 (over y), dp: 8 (over x, core).
Axes of the slice: x: 4, y: 4, z: 8, core: 2. Of those that a mesh axis runs over, the one named last changes fastest.
Arguments:
- tok_in: bfloat16 [98304, 384], P(('rep', 'ep', 'dp'))
- tok_grad: bfloat16 [98304, 384], P(('rep', 'ep', 'dp'))
- route_ids: int32 [2, 98304, 2], P(None, ('rep', 'ep', 'dp'))
- gate_vals: float32 [2, 98304, 2], P(None, ('rep', 'ep', 'dp'))
- w_dense: bfloat16 [2, 384, 384], replicated
- w_gate: bfloat16 [2, 8, 384, 2048], P(None, 'ep')
- w_up: bfloat16 [2, 8, 384, 2048], P(None, 'ep')
- w_down: bfloat16 [2, 8, 2048, 384], P(None, 'ep')
Outputs:
- output 1: bfloat16 [98304, 384], P(('rep', 'ep', 'dp'))
- output 2: bfloat16 [98304, 384], P(('rep', 'ep', 'dp'))
- output 3: bfloat16 [2, 384, 384], replicated
- output 4: bfloat16 [2, 8, 384, 2048], P(None, 'ep')
- output 5: bfloat16 [2, 8, 384, 2048], P(None, 'ep')
- output 6: bfloat16 [2, 8, 2048, 384], P(None, 'ep')
All inputs are finite; a program needn't handle non-finite values.
Results may differ from a plain program's by a relative error of at most 0.02.
Values are sent between devices in bfloat16 or wider.
A program may use at most 768 MiB of HBM per device.

v0:
```python
import jax
import jax.numpy as jnp
from jax import lax
from jax.sharding import PartitionSpec as P

TOK_AXES = ("rep", "ep", "dp")


def slot_tables(route_loc, experts):
    tokens, top_k = route_loc.shape
    capacity = 2 * tokens * top_k // experts
    flat_ids = route_loc.reshape(tokens * top_k)
    expert_hits = (flat_ids[:, None] == jnp.arange(experts, dtype=jnp.int32)[None, :]).astype(jnp.int32)
    slot_rank = jnp.sum((jnp.cumsum(expert_hits, axis=0) - 1) * expert_hits, axis=1)
    slot_of = flat_ids * capacity + slot_rank
    copy_of = jnp.full((experts * capacity,), tokens * top_k, jnp.int32)
    copy_of = copy_of.at[slot_of].set(jnp.arange(tokens * top_k, dtype=jnp.int32))
    return slot_of, copy_of


def layer_forward(tok_loc, route_loc, gate_loc, dense_w, gate_w, up_w, down_w, ep_size):
    tokens, top_k = route_loc.shape
    model_width = tok_loc.shape[1]
    experts = gate_w.shape[0] * ep_size
    capacity = 2 * tokens * top_k // experts
    mixed_val = (tok_loc.astype(jnp.float32) + jnp.dot(tok_loc, dense_w, preferred_element_type=jnp.float32)).astype(jnp.bfloat16)
    slot_of, copy_of = slot_tables(route_loc, experts)
    padded = jnp.concatenate([mixed_val, jnp.zeros((1, model_width), jnp.bfloat16)], axis=0)
    send_buf = jnp.take(padded, copy_of // top_k, axis=0).reshape(experts, capacity, model_width)
    expert_in = lax.all_to_all(send_buf, "ep", 0, 1, tiled=True)
    act_gate = jnp.einsum("end,edf->enf", expert_in, gate_w, preferred_element_type=jnp.float32).astype(jnp.bfloat16)
    act_up = jnp.einsum("end,edf->enf", expert_in, up_w, preferred_element_type=jnp.float32).astype(jnp.bfloat16)
    hidden = (jax.nn.silu(act_gate.astype(jnp.float32)) * act_up.astype(jnp.float32)).astype(jnp.bfloat16)
    expert_out = jnp.einsum("enf,efd->end", hidden, down_w, preferred_element_type=jnp.float32).astype(jnp.bfloat16)
    returned = lax.all_to_all(expert_out, "ep", 1, 0, tiled=True).reshape(experts * capacity, model_width)
    per_copy = jnp.take(returned, slot_of, axis=0).reshape(tokens, top_k, model_width)
    mix_sum = jnp.sum(gate_loc[:, :, None] * per_copy, axis=1)
    tok_out = (mixed_val.astype(jnp.float32) + mix_sum).astype(jnp.bfloat16)
    return tok_out, (tok_loc, slot_of, copy_of, expert_in, act_gate, act_up, hidden)


def layer_backward(grad_out, gate_loc, dense_w, gate_w, up_w, down_w, layer_saved, ep_size):
    tok_loc, slot_of, copy_of, expert_in, act_gate, act_up, hidden = layer_saved
    tokens, top_k = gate_loc.shape
    model_width = grad_out.shape[1]
    experts = gate_w.shape[0] * ep_size
    capacity = copy_of.shape[0] // experts
    gate_pad = jnp.concatenate([gate_loc.reshape(tokens * top_k), jnp.zeros((1,), jnp.float32)])
    grad_pad = jnp.concatenate([grad_out, jnp.zeros((1, model_width), jnp.bfloat16)], axis=0)
    slot_gate = jnp.take(gate_pad, copy_of)
    send_grad = (slot_gate[:, None] * jnp.take(grad_pad, copy_of // top_k, axis=0)).astype(jnp.bfloat16).reshape(experts, capacity, model_width)
    grad_exp_out = lax.all_to_all(send_grad, "ep", 0, 1, tiled=True)
    grad_hidden = jnp.einsum("end,efd->enf", grad_exp_out, down_w, preferred_element_type=jnp.float32)
    grad_down = jnp.einsum("enf,end->efd", hidden, grad_exp_out, preferred_element_type=jnp.float32)
    gate_f = act_gate.astype(jnp.float32)
    sig_gate = jax.nn.sigmoid(gate_f)
    grad_up_act = (grad_hidden * gate_f * sig_gate).astype(jnp.bfloat16)
    grad_gate_act = (grad_hidden * act_up.astype(jnp.float32) * sig_gate * (1.0 + gate_f * (1.0 - sig_gate))).astype(jnp.bfloat16)
    grad_gate = jnp.einsum("end,enf->edf", expert_in, grad_gate_act, preferred_element_type=jnp.float32)
    grad_up = jnp.einsum("end,enf->edf", expert_in, grad_up_act, preferred_element_type=jnp.float32)
    grad_exp_in = (jnp.einsum("enf,edf->end", grad_gate_act, gate_w, preferred_element_type=jnp.float32) + jnp.einsum("enf,edf->end", grad_up_act, up_w, preferred_element_type=jnp.float32)).astype(jnp.bfloat16)
    grad_back = lax.all_to_all(grad_exp_in, "ep", 1, 0, tiled=True).reshape(experts * capacity, model_width)
    grad_mixed = grad_out.astype(jnp.float32) + jnp.sum(jnp.take(grad_back, slot_of, axis=0).reshape(tokens, top_k, model_width), axis=1, dtype=jnp.float32)
    grad_mixed_bf = grad_mixed.astype(jnp.bfloat16)
    grad_dense = lax.dot_general(tok_loc, grad_mixed_bf, (((0,), (0,)), ((), ())), preferred_element_type=jnp.float32)
    grad_tok = (grad_mixed + lax.dot_general(grad_mixed_bf, dense_w, (((1,), (1,)), ((), ())), preferred_element_type=jnp.float32)).astype(jnp.bfloat16)
    return grad_tok, grad_dense, grad_gate, grad_up, grad_down


def solution(mesh):
    ep_size = mesh.shape["ep"]
    tok_spec = P(TOK_AXES, None)
    route_spec = P(None, TOK_AXES, None)
    expert_spec = P(None, "ep", None, None)
    whole_spec = P(None, None, None)

    def device_step(tok_in, tok_grad, route_ids, gate_vals, w_dense, w_gate, w_up, w_down):
        layers = w_dense.shape[0]
        current = tok_in
        saved_all = []
        for layer_idx in range(layers):
            current, layer_saved = layer_forward(current, route_ids[layer_idx], gate_vals[layer_idx], w_dense[layer_idx], w_gate[layer_idx], w_up[layer_idx], w_down[layer_idx], ep_size)
            saved_all.append(layer_saved)
        grad_cur = tok_grad
        dense_sums = []
        gate_sums = []
        up_sums = []
        down_sums = []
        for layer_idx in reversed(range(layers)):
            grad_cur, grad_dense, grad_gate, grad_up, grad_down = layer_backward(grad_cur, gate_vals[layer_idx], w_dense[layer_idx], w_gate[layer_idx], w_up[layer_idx], w_down[layer_idx], saved_all[layer_idx], ep_size)
            dense_sums.insert(0, lax.psum(grad_dense.astype(jnp.bfloat16), TOK_AXES))
            gate_sums.insert(0, lax.psum(lax.psum(grad_gate.astype(jnp.bfloat16), "rep"), "dp"))
            up_sums.insert(0, lax.psum(lax.psum(grad_up.astype(jnp.bfloat16), "rep"), "dp"))
            down_sums.insert(0, lax.psum(lax.psum(grad_down.astype(jnp.bfloat16), "rep"), "dp"))
        return current, grad_cur, jnp.stack(dense_sums), jnp.stack(gate_sums), jnp.stack(up_sums), jnp.stack(down_sums)

    return jax.shard_map(device_step, mesh=mesh, in_specs=(tok_spec, tok_spec, route_spec, route_spec, whole_spec, expert_spec, expert_spec, expert_spec), out_specs=(tok_spec, tok_spec, whole_spec, expert_spec, expert_spec, expert_spec), check_vma=False)
```

profile of v0, /device:TPU:1, one launch (start us, length us, event | category | flops | bytes accessed | tf_op | source)
XLA Modules:
  0.0 1157.4 jit_solution(18227463456343869018)
XLA Ops:
  15.9 4.7 gather_fusion
  22.0 5.0 all-to-all-start
  36.9 4.8 all-to-all-done
  41.8 6.0 convolution_convert_fusion.3
  48.0 10.6 fusion
  68.7 5.9 gather_fusion.4
  74.6 4.7 gather_fusion.5
  81.3 4.5 all-to-all-start.4
  93.9 5.0 gather_fusion.2
  104.4 5.9 gather_fusion.7
  111.7 4.5 all-to-all-done.2
  116.4 7.7 convolution_convert_fusion
  124.1 7.4 convolution_convert_fusion.1
  131.4 15.2 %fusion.7 = (bf16[2,768,2048]{2,1,0:T(8,128)(2,1)}, bf16[2,768,2048]{2,1,0:T(8,128)(2,1)}, bf16[2,768,2048]{2,1,0:T(8,128)(2,1)}) fusion(bf16[2,768,2048]{2,1,0:T(8,128)(2,1)} %convolution_convert_fusion, bf16[2,768,2048]{2,1,0:T(8,128)(2,1)} %convolution_convert_fusion.1, bf16[2,768,384]{2,1,0:T(8,128)(2,1)S(1)} %bitcast.175, ...), kind=kOutput, calls=%fused_computation.31 | convolution fusion | flops 2472542208 | bytes 35782656 | tf_op jit(solution)/shard_map/end,efd->enf/dot_general | solution.py:53
  146.6 6.2 fusion.59
  158.8 6.5 fusion.24
  165.3 7.2 add_convert_fusion.1
  174.7 4.7 all-to-all-start.5
  180.0 8.0 convolution_convert_fusion.4
  201.7 4.7 gather_fusion.8
  212.1 7.6 convolution_convert_fusion.6
  219.7 7.1 convolution_convert_fusion.8
  227.0 7.9 convolution_convert_fusion.5
  234.9 12.7 %fusion.3 = (bf16[2,768,2048]{2,1,0:T(8,128)(2,1)S(1)}, bf16[2,768,2048]{2,1,0:T(8,128)(2,1)}) fusion(bf16[2,768,2048]{2,1,0:T(8,128)(2,1)} %get-tuple-element.65, bf16[2,768,2048]{2,1,0:T(8,128)(2,1)} %copy-done.35, bf16[2,768,384]{2,1,0:T(8,128)(2,1)S(1)} %bitcast.178, bf16[2,2,2048,384]{3,2,1,0:T(8,128)(2,1)} %param.21), kind=kOutput, calls=%fused_computation.27 | convolution fusion | flops 2463105024 | bytes 29491200 | tf_op jit(solution)/shard_map/end,efd->enf/dot_general | solution.py:53
  247.6 9.4 convolution_convert_fusion.7
  261.1 6.9 fusion.34
  268.0 5.3 add_convert_fusion
  280.9 9.1 all-to-all-done.7
  296.6 360.7 %all-reduce.15.cloned.1.call-done = (bf16[2,384,2048]{2,1,0:T(8,128)(2,1)}, bf16[2,384,2048]{2,1,0:T(8,128)(2,1)}, bf16[2,384,2048]{2,1,0:T(8,128)(2,1)}, bf16[2...) async-done(((bf16[2,384,2048]{2,1,0:T(8,128)(2,1)}, bf16[2,384,2048]{2,1,0:T(8,128)(2,1)}, bf16[2,384,2048]{2,1,0:T(8,128)(2,1)}, ...) | async-done | bytes 18874384 | tf_op jit(solution)/shard_map/psum | solution.py:92
  663.8 261.1 %all-reduce.11.cloned.1.call-done = (bf16[1,384,384]{1,2,0:T(8,128)(2,1)}, bf16[1,384,384]{1,2,0:T(8,128)(2,1)}) async-done(((bf16[1,384,384]{1,2,0:T(8,128)(2,1)}, bf16[1,384,384]{1,2,0:T(8,128)(2,1)}), (bf16[1,384,384]{1,2,0:T(8,128)(2,1)}, bf16[1,384,384]{1,2,0:T(8,128)(2,1)})) %all-reduce.11.cloned.1.call-update) | async-done | bytes 589840 | tf_op jit(solution)/shard_map/psum | solution.py:91
  927.1 208.6 %all-reduce.13.cloned.1.call-done = (bf16[1,2,384,2048]{3,2,1,0:T(8,128)(2,1)}, bf16[1,2,384,2048]{3,2,1,0:T(8,128)(2,1)}, bf16[1,2,384,2048]{3,2,1,0:T(8,128)(2...) async-done(((bf16[1,2,384,2048]{3,2,1,0:T(8,128)(2,1)}, bf16[1,2,384,2048]{3,2,1,0:T(8,128)(2,1)}, ...) | async-done | bytes 18874384 | tf_op jit(solution)/shard_map/psum | solution.py:92
  1135.8 6.3 pad_maximum_fusion
  (205 shorter events, 110.6 us)
Async XLA Ops:
  14.3 6.3 copy-start.27
  14.4 6.3 copy-start.19
  15.9 76.6 %copy-start.6 = (bf16[384,384]{1,0:T(8,128)(2,1)}, bf16[384,384]{1,0:T(8,128)(2,1)S(1)}, u32[]{:S(2)}) copy-start(bf16[384,384]{1,0:T(8,128)(2,1)S(1)} %fusion.62) | copy-start | bytes 884740
  20.6 6.8 copy-start.34
  22.0 19.7 %all-to-all-start = ((bf16[8,192,384]{2,1,0:T(8,128)(2,1)}), bf16[8,192,384]{2,1,0:T(8,128)(2,1)S(1)}, u32[]{:S(2)}, u32[]{:S(2)}) async-start(bf16[8,192,384]{2,1,0:T(8,128)(2,1)} %bitcast.5), calls=%async_computation | async-start | bytes 2359296 | tf_op jit(solution)/shard_map/all_to_all | solution.py:30
  27.3 20.6 %copy-start.22 = (s32[768]{0:T(1024)}, s32[768]{0:T(1024)S(1)}, u32[]{:S(2)}) copy-start(s32[768]{0:T(1024)S(1)} %eq.58) | copy-start | bytes 9220
  31.1 16.7 %copy-start.24 = (s32[768]{0:T(1024)}, s32[768]{0:T(1024)S(1)}, u32[]{:S(2)}) copy-start(s32[768]{0:T(1024)S(1)} %fusion.82) | copy-start | bytes 9220
  35.1 12.8 %copy-start.17 = (s32[1536]{0:T(1024)}, s32[1536]{0:T(1024)S(1)}, u32[]{:S(2)}) copy-start(s32[1536]{0:T(1024)S(1)} %scatter_custom_fusion.1) | copy-start | bytes 18436
  41.8 16.7 %slice-start = ((s8[6291456]{0:T(1024)(128)(4,1)}), s8[4194304]{0:T(1024)(128)(4,1)S(1)}, s32[]{:S(2)}) async-start(s8[6291456]{0:T(1024)(128)(4,1)} %bitcast.183), calls=%async_computation.11 | async-start | bytes 8388608
  47.9 10.6 copy-start.35
  47.9 10.6 slice-start.1
  62.0 6.6 copy-start.5
  64.2 17.0 %all-to-all-start.1 = ((bf16[2,768,384]{2,0,1:T(2,128)(2,1)}), bf16[2,768,384]{2,0,1:T(2,128)(2,1)S(1)}, u32[]{:S(2)}, u32[]{:S(2)}) async-start(bf16[2,768,384]{2,0,1:T(2,128)(2,1)} %copy.69), calls=%async_computation.1 | async-start | bytes 2359296 | tf_op jit(solution)/shard_map/all_to_all | solution.py:35
  81.3 18.9 %all-to-all-start.4 = ((bf16[8,192,384]{2,1,0:T(8,128)(2,1)}), bf16[8,192,384]{2,1,0:T(8,128)(2,1)}, u32[]{:S(2)}, u32[]{:S(2)}) async-start(bf16[8,192,384]{2,1,0:T(8,128)(2,1)} %bitcast.160), calls=%async_computation.4 | async-start | bytes 2359296 | tf_op jit(solution)/shard_map/all_to_all | solution.py:52
  100.2 16.0 %all-to-all-start.2 = ((bf16[8,192,384]{2,1,0:T(8,128)(2,1)}), bf16[8,192,384]{2,1,0:T(8,128)(2,1)S(1)}, u32[]{:S(2)}, u32[]{:S(2)}) async-start(bf16[8,192,384]{2,1,0:T(8,128)(2,1)} %bitcast.20), calls=%async_computation.2 | async-start | bytes 2359296 | tf_op jit(solution)/shard_map/all_to_all | solution.py:30
  116.3 7.7 copy-start.14
  116.3 15.1 %slice-start.2 = ((s8[6291456]{0:T(1024)(128)(4,1)}), s8[4194304]{0:T(1024)(128)(4,1)S(1)}, s32[]{:S(2)}) async-start(s8[6291456]{0:T(1024)(128)(4,1)} %bitcast.185), calls=%async_computation.13 | async-start | bytes 8388608
  124.1 7.4 slice-start.3
  155.1 19.6 %all-to-all-start.3 = ((bf16[2,768,384]{2,0,1:T(2,128)(2,1)}), bf16[2,768,384]{2,0,1:T(2,128)(2,1)S(1)}, u32[]{:S(2)}, u32[]{:S(2)}) async-start(bf16[2,768,384]{2,0,1:T(2,128)(2,1)} %copy.78), calls=%async_computation.3 | async-start | bytes 2359296 | tf_op jit(solution)/shard_map/all_to_all | solution.py:35
  174.7 14.9 %all-to-all-start.5 = ((bf16[2,768,384]{2,0,1:T(2,128)(2,1)}), bf16[2,768,384]{2,0,1:T(2,128)(2,1)}, u32[]{:S(2)}, u32[]{:S(2)}) async-start(bf16[2,768,384]{2,0,1:T(2,128)(2,1)} %copy.82), calls=%async_computation.5 | async-start | bytes 2359296 | tf_op jit(solution)/shard_map/all_to_all | solution.py:62
  208.3 18.5 %all-to-all-start.6 = ((bf16[8,192,384]{2,1,0:T(8,128)(2,1)}), bf16[8,192,384]{2,1,0:T(8,128)(2,1)S(1)}, u32[]{:S(2)}, u32[]{:S(2)}) async-start(bf16[8,192,384]{2,1,0:T(8,128)(2,1)} %bitcast.37), calls=%async_computation.6 | async-start | bytes 2359296 | tf_op jit(solution)/shard_map/all_to_all | solution.py:52
  211.9 445.4 %all-reduce.15.cloned.1.call-start = ((), (), s32[]{:S(2)}) async-start(), calls=%async_computation.10 | async-start | bytes 37748736 | tf_op jit(solution)/shard_map/psum | solution.py:92
  212.1 7.6 copy-start.15
  234.9 12.7 %copy-start.13 = (bf16[2,4,192,384]{3,2,1,0:T(8,128)(2,1)S(1)}, bf16[2,4,192,384]{3,2,1,0:T(8,128)(2,1)}, u32[]{:S(2)}) copy-start(bf16[2,4,192,384]{3,2,1,0:T(8,128)(2,1)} %copy-done.12) | copy-start | bytes 3538948
  247.6 9.4 copy-start.37
  261.1 6.9 copy-start.38
  273.4 6.4 copy-start.7
  275.6 14.4 %all-to-all-start.7 = ((bf16[2,768,384]{2,0,1:T(2,128)(2,1)}), bf16[2,768,384]{2,0,1:T(2,128)(2,1)S(1)}, u32[]{:S(2)}, u32[]{:S(2)}) async-start(bf16[2,768,384]{2,0,1:T(2,128)(2,1)} %copy.86), calls=%async_computation.7 | async-start | bytes 2359296 | tf_op jit(solution)/shard_map/all_to_all | solution.py:62
  279.8 645.2 %all-reduce.11.cloned.1.call-start = ((), (), s32[]{:S(2)}) async-start(), calls=%async_computation.8 | async-start | bytes 1179648 | tf_op jit(solution)/shard_map/psum | solution.py:91
  296.2 839.5 %all-reduce.13.cloned.1.call-start = ((), (), s32[]{:S(2)}) async-start(), calls=%async_computation.9 | async-start | bytes 37748736 | tf_op jit(solution)/shard_map/psum | solution.py:92
  1135.7 6.3 copy-start.3
  1135.8 6.3 copy-start.4
  (22 other events, 91.0 us)
Sparse Core Ops, SparseCore 0:
  261.2 396.0 all-reduce.14
  663.5 261.4 all-reduce.10
  928.1 207.6 all-reduce.12
where the time goes:
time: 1160 us
  waiting for transfers between devices  850 us (73%)
  matrix products  147 us (13%)
  local copies, waits for them, and re-layouts  72.8 us (6%)
  other arithmetic  38.7 us (3%)
  starting transfers between devices  33.9 us (3%)
  between operations  15.1 us (1%)
    psum x1, waiting for transfers between devices, device_step(): lax.psum(grad_gate.astype(jnp.bfloat16), 'rep')  361 us
    psum x1, waiting for transfers between devices, device_step(): dense_sums.insert(0, lax.psum(grad_dense.astype(jnp.bfloat16), TOK_AXES))  261 us
    psum x1, waiting for transfers between devices, device_step(): lax.psum(lax.psum(grad_gate.astype(jnp.bfloat16), 'rep'), 'dp')  209 us
    dot_general x2, matrix products, layer_backward(): jnp.einsum('end,efd->enf', grad_exp_out, down_w, preferred_element_type=j...  27.8 us
  transfers between devices with their start and end apart: 11, of which 7 were waited for; matrix products, arithmetic and copies ran while one was open for 10% of the time, Pallas kernels for 0%

commit v1 on v0

v1 whole, which is shorter than its diff:
```python
import jax
import jax.numpy as jnp
from jax import lax
from jax.experimental import pallas as pl
from jax.experimental.pallas import tpu as pltpu
from jax.sharding import PartitionSpec as P

TOK_AXES = ("rep", "ep", "dp")
COPY_AXES = ("rep", "dp")
F32 = jnp.float32
BF16 = jnp.bfloat16


def mm(a, b, dims):
    return lax.dot_general(a, b, (dims, ((), ())), preferred_element_type=F32)


LANES = 128
STEP = 16


def shard_copies(local_shards, half, low):
    for k in range(local_shards):
        rows, cols = slice((k % 2) * half, (k % 2 + 1) * half), slice(k // 2 * LANES, (k // 2 + 1) * LANES)
        yield k, 0, half, rows, cols
        yield k, 1, half, rows, cols
        for c in range(half // low):
            yield k, 2 + c, low, slice(k * low, (k + 1) * low), slice(c * LANES, (c + 1) * LANES)


def pack_kernel(half, low, gate_ref, up_ref, down_ref, out_ref):
    for k, piece, size, rows, cols in shard_copies(STEP, half, low):
        src = (gate_ref, up_ref, down_ref)[min(piece, 2)]
        at = piece * half if piece < 2 else 2 * half + (piece - 2) * low
        out_ref[k, at : at + size, :] = src[0, rows, cols]


def unpack_kernel(half, low, in_ref, *refs):
    gate_ref, up_ref, down_ref = refs[-3:]
    for k, piece, size, rows, cols in shard_copies(STEP, half, low):
        dst = (gate_ref, up_ref, down_ref)[min(piece, 2)]
        at = piece * half if piece < 2 else 2 * half + (piece - 2) * low
        dst[0, 0, rows, cols] = in_ref[k, at : at + size, :]


def pack(gate, up, down):
    local, width, ff = gate.shape
    shards = 2 * local * ff // LANES
    half, low = width // 2, local * ff // shards
    per = shards // local // STEP
    wide = pl.BlockSpec((1, width, STEP // 2 * LANES), lambda i: (i // per, 0, i % per))
    tall = pl.BlockSpec((1, STEP * low, width), lambda i: (i // per, i % per, 0))
    rows = 2 * half + width // LANES * low
    return pl.pallas_call(
        lambda *refs: pack_kernel(half, low, *refs),
        grid=(shards // STEP,),
        in_specs=[wide, wide, tall],
        out_specs=pl.BlockSpec((STEP, rows, LANES), lambda i: (i, 0, 0)),
        out_shape=jax.ShapeDtypeStruct((shards, rows, LANES), BF16),
        cost_estimate=pl.CostEstimate(flops=10**8, bytes_accessed=4 * gate.size * 3, transcendentals=0),
        name="pack",
    )(gate, up, down)


def unpack(packed, layer, shapes, into):
    (layers, local, width, ff), shards = shapes[0], packed.shape[0]
    half, low = width // 2, local * ff // shards
    per = shards // local // STEP
    wide = pl.BlockSpec((1, 1, width, STEP // 2 * LANES), lambda i: (layer, i // per, 0, i % per))
    tall = pl.BlockSpec((1, 1, STEP * low, width), lambda i: (layer, i // per, i % per, 0))
    return pl.pallas_call(
        lambda *refs: unpack_kernel(half, low, *refs),
        grid=(shards // STEP,),
        in_specs=[pl.BlockSpec((STEP, packed.shape[1], LANES), lambda i: (i, 0, 0))] + [pl.BlockSpec(memory_space=pl.ANY)] * len(into),
        out_specs=[wide, wide, tall],
        out_shape=[jax.ShapeDtypeStruct(s, BF16) for s in shapes],
        input_output_aliases={1 + i: i for i in range(len(into))},
        cost_estimate=pl.CostEstimate(flops=10**8, bytes_accessed=4 * packed.size, transcendentals=0),
        name=f"unpack_{layer}",
    )(packed, *into)


def slot_tables(route_loc, experts):
    tokens, top_k = route_loc.shape
    capacity = 2 * tokens * top_k // experts
    hits = (route_loc[:, :, None] == jnp.arange(experts, dtype=jnp.int32)).astype(BF16)
    token_hits = jnp.sum(hits, axis=1)
    order = (jnp.arange(tokens)[:, None] > jnp.arange(tokens)[None, :]).astype(BF16)
    before = mm(order, token_hits, ((1,), (0,)))
    rank = jnp.sum(before[:, None, :] * hits.astype(F32), axis=2).astype(jnp.int32)
    slot_of = route_loc * capacity + rank
    slots = jnp.arange(experts * capacity, dtype=jnp.int32)
    return (slots[None, :, None] == slot_of.T[:, None, :]).astype(BF16)


def layer_forward(tok_loc, pick, gate_loc, dense_w, gate_w, up_w, down_w, ep_size):
    tokens, top_k = gate_loc.shape
    model_width = tok_loc.shape[1]
    experts = gate_w.shape[0] * ep_size
    capacity = 2 * tokens * top_k // experts
    mixed_val = (tok_loc.astype(F32) + mm(tok_loc, dense_w, ((1,), (0,)))).astype(BF16)
    send_buf = mm(pick[0] + pick[1], mixed_val, ((1,), (0,))).astype(BF16).reshape(experts, capacity, model_width)
    expert_in = lax.all_to_all(send_buf, "ep", 0, 1, tiled=True)
    act_gate = jnp.einsum("end,edf->enf", expert_in, gate_w, preferred_element_type=F32).astype(BF16)
    act_up = jnp.einsum("end,edf->enf", expert_in, up_w, preferred_element_type=F32).astype(BF16)
    hidden = (jax.nn.silu(act_gate.astype(F32)) * act_up.astype(F32)).astype(BF16)
    expert_out = jnp.einsum("enf,efd->end", hidden, down_w, preferred_element_type=F32).astype(BF16)
    returned = lax.all_to_all(expert_out, "ep", 1, 0, tiled=True).reshape(experts * capacity, model_width)
    mix_sum = gate_loc[:, 0:1] * mm(pick[0], returned, ((0,), (0,))) + gate_loc[:, 1:2] * mm(pick[1], returned, ((0,), (0,)))
    tok_out = (mixed_val.astype(F32) + mix_sum).astype(BF16)
    return tok_out, (tok_loc, expert_in, act_gate, act_up, hidden)


def send_gradient(grad_out, pick, gate_loc, experts):
    slots, tokens = pick.shape[1:]
    grad_f = grad_out.astype(F32)
    scaled = jnp.concatenate([(gate_loc[:, 0:1] * grad_f).astype(BF16), (gate_loc[:, 1:2] * grad_f).astype(BF16)], axis=0)
    both = jnp.concatenate([pick[0], pick[1]], axis=1)
    rows = mm(both, scaled, ((1,), (0,))).astype(BF16)
    return lax.all_to_all(rows.reshape(experts, slots // experts, grad_out.shape[1]), "ep", 0, 1, tiled=True)


def layer_backward(grad_out, grad_exp_out, pick, dense_w, gate_w, up_w, down_w, layer_saved, ep_size, gathered):
    tok_loc, expert_in, act_gate, act_up, hidden = layer_saved
    model_width = grad_out.shape[1]
    grad_hidden = jnp.einsum("end,efd->enf", grad_exp_out, down_w, preferred_element_type=F32)
    gate_f = act_gate.astype(F32)
    sig_gate = jax.nn.sigmoid(gate_f)
    grad_up_act = (grad_hidden * gate_f * sig_gate).astype(BF16)
    grad_gate_act = (grad_hidden * act_up.astype(F32) * sig_gate * (1.0 + gate_f * (1.0 - sig_gate))).astype(BF16)
    grad_exp_in = (jnp.einsum("enf,edf->end", grad_gate_act, gate_w, preferred_element_type=F32) + jnp.einsum("enf,edf->end", grad_up_act, up_w, preferred_element_type=F32)).astype(BF16)
    grad_back = lax.all_to_all(grad_exp_in, "ep", 1, 0, tiled=True).reshape(pick.shape[1], model_width)
    grad_down = jnp.einsum("enf,end->efd", hidden, grad_exp_out, preferred_element_type=F32).astype(BF16)
    grad_gate = jnp.einsum("end,enf->edf", expert_in, grad_gate_act, preferred_element_type=F32).astype(BF16)
    grad_up = jnp.einsum("end,enf->edf", expert_in, grad_up_act, preferred_element_type=F32).astype(BF16)
    packed = pack(grad_gate, grad_up, grad_down)
    if gathered is not None:
        packed, gathered = lax.optimization_barrier((packed, gathered))
    summed = lax.psum_scatter(packed, COPY_AXES, scatter_dimension=0, tiled=False)
    grad_mixed = grad_out.astype(F32) + mm(pick[0] + pick[1], grad_back, ((0,), (0,)))
    grad_mixed_bf = grad_mixed.astype(BF16)
    grad_dense = mm(tok_loc, grad_mixed_bf, ((0,), (0,))).astype(BF16)
    grad_tok = (grad_mixed + mm(grad_mixed_bf, dense_w, ((1,), (1,)))).astype(BF16)
    return grad_tok, grad_dense, summed, gathered


def sum_dense(grads):
    rows, width = grads.shape
    part = grads
    for axis in ("dp", "rep"):
        pieces = lax.all_to_all(part.reshape(lax.axis_size(axis), -1, width), axis, 0, 0, tiled=True)
        part = jnp.sum(pieces.astype(F32), axis=0).astype(BF16)
    part = jnp.sum(lax.all_gather(part, "ep", axis=0).astype(F32), axis=0).astype(BF16)
    for axis in ("rep", "dp"):
        part = lax.all_gather(part, axis, axis=0, tiled=True)
    return part


def solution(mesh):
    ep_size = mesh.shape["ep"]
    tok_spec = P(TOK_AXES, None)
    route_spec = P(None, TOK_AXES, None)
    expert_spec = P(None, "ep", None, None)
    whole_spec = P(None, None, None)

    def device_step(tok_in, tok_grad, route_ids, gate_vals, w_dense, w_gate, w_up, w_down):
        layers, model_width = w_dense.shape[:2]
        local, ff = w_gate.shape[1], w_gate.shape[3]
        experts = local * ep_size
        picks = [slot_tables(route_ids[i], experts) for i in range(layers)]
        current = tok_in
        saved_all = []
        for i in range(layers):
            current, layer_saved = layer_forward(current, picks[i], gate_vals[i], w_dense[i], w_gate[i], w_up[i], w_down[i], ep_size)
            saved_all.append(layer_saved)
        grad_cur = tok_grad
        dense, summed, gathered, grads = [None] * layers, None, None, ()
        shapes = [w_gate.shape, w_up.shape, w_down.shape]
        for i in reversed(range(layers)):
            sent = send_gradient(grad_cur, picks[i], gate_vals[i], experts)
            if summed is not None:
                sent, summed = lax.optimization_barrier((sent, summed))
                gathered = lax.all_gather(summed, COPY_AXES, axis=0)
            grad_cur, dense[i], summed, gathered = layer_backward(grad_cur, sent, picks[i], w_dense[i], w_gate[i], w_up[i], w_down[i], saved_all[i], ep_size, gathered)
            if gathered is not None:
                grads = unpack(gathered, i + 1, shapes, grads)
        grad_cur, dense, current, summed = lax.optimization_barrier((grad_cur, dense, current, summed))
        grad_dense = sum_dense(jnp.concatenate(dense, axis=0)).reshape(layers, model_width, model_width)
        grads = unpack(lax.all_gather(summed, COPY_AXES, axis=0), 0, shapes, grads)
        return current, grad_cur, grad_dense, *grads

    return jax.shard_map(device_step, mesh=mesh, in_specs=(tok_spec, tok_spec, route_spec, route_spec, whole_spec, expert_spec, expert_spec, expert_spec), out_specs=(tok_spec, tok_spec, whole_spec, expert_spec, expert_spec, expert_spec), check_vma=False)
```

time: 1160 us -> 680 us (0.59)
  waiting for transfers between devices: 850 us -> 318 us
  blocking collectives: 0 us -> 84.4 us
  local copies, waits for them, and re-layouts: 72.8 us -> 31.8 us
  Pallas kernels: 0 us -> 32.8 us
  other arithmetic: 38.7 us -> 7.29 us
    psum x3 -> x0, waiting for transfers between devices: 830 us -> none  [the longest x1 361 us: device_step(): lax.psum(grad_gate.astype(jnp.bfloat16), 'rep')]
    unnamed x3 -> x6, waiting for transfers between devices: 0.05 us -> 209 us
    all_gather x0 -> x2, waiting for transfers between devices: none -> 56.2 us  [the longest x1 51.6 us: device_step(): gathered = lax.all_gather(summed, COPY_AXES, axis=0)]
    all_gather x0 -> x3, blocking collectives: none -> 52.6 us  [the longest x2 42.9 us: sum_dense(): part = lax.all_gather(part, axis, axis=0, tiled=True)]
    gather x10 -> x0, local copies, waits for them, and re-layouts: 41.9 us -> none  [the longest x2 11.7 us: layer_backward(): slot_gate = jnp.take(gate_pad, copy_of)]
    pallas_call x0 -> x4, Pallas kernels: none -> 32.8 us  [the longest x2 16.8 us: unpack(): pl.pallas_call(lambda *refs: unpack_kernel(half, low, *refs), grid=(shard...]
    all_to_all x0 -> x2, blocking collectives: none -> 31.8 us  [the longest x1 18.9 us: sum_dense(): lax.all_to_all(part.reshape(lax.axis_size(axis), -1, width), axis, 0, 0,...]
    another operation x8 -> x0, other arithmetic: 18.2 us -> none  [the longest x1 6.26 us: device_step(): jnp.stack(gate_sums)]
  transfers between devices with their start and end apart: 11 -> 12, of which waited for: 7 -> 10; matrix products, arithmetic and copies ran while one was open for 10% -> 15% of each run, Pallas kernels for 0% -> 2%
where the time goes in v1:
time: 680 us; the launch traced here: 670 us
  waiting for transfers between devices  318 us (47%)
  matrix products  148 us (22%)
  blocking collectives  84.4 us (12%)
  starting transfers between devices  33.6 us (5%)
  Pallas kernels  32.8 us (5%)
  local copies, waits for them, and re-layouts  31.8 us (5%)
  between operations  14.8 us (2%)
  other arithmetic  7.29 us (1%)
    unnamed x6, waiting for transfers between devices  209 us
    all_gather x1, waiting for transfers between devices, device_step(): gathered = lax.all_gather(summed, COPY_AXES, axis=0)  51.6 us
    all_gather x2, blocking collectives, sum_dense(): part = lax.all_gather(part, axis, axis=0, tiled=True)  42.9 us
    dot_general x2, matrix products, layer_backward(): jnp.einsum('end,efd->enf', grad_exp_out, down_w, preferred_element_type=F32)  29.6 us
    all_to_all x2, waiting for transfers between devices, layer_forward(): expert_in = lax.all_to_all(send_buf, 'ep', 0, 1, tiled=True)  21 us
    all_to_all x1, blocking collectives, sum_dense(): lax.all_to_all(part.reshape(lax.axis_size(axis), -1, width), axis, 0, 0,...  18.9 us
    all_to_all x2, waiting for transfers between devices, layer_backward(): lax.all_to_all(grad_exp_in, 'ep', 1, 0, tiled=True)  18.4 us
    dot_general x18, matrix products, mm(): return lax.dot_general(a, b, (dims, ((), ())), preferred_element_type=F32)  18.1 us
  transfers between devices with their start and end apart: 12, of which 10 were waited for; matrix products, arithmetic and copies ran while one was open for 15% of the time, Pallas kernels for 2%

profile of v1, /device:TPU:1, one launch (start us, length us, event | category | flops | bytes accessed | tf_op | source)
XLA Modules:
  0.0 670.1 jit_solution(2344025823980339079)
XLA Ops:
  14.3 5.0 all-to-all-start.1
  22.8 11.2 %all-to-all-done.1 = bf16[8,192,384]{2,1,0:T(8,128)(2,1)S(1)} async-done(((bf16[8,192,384]{2,1,0:T(8,128)(2,1)}), bf16[8,192,384]{2,1,0:T(8,128)(2,1)S(1)}, u32[]{:S(2)}, u32[]{:S(2)}) %all-to-all-start.1) | async-done | bytes 1179680 | tf_op jit(solution)/shard_map/all_to_all | solution.py:103
  34.2 6.0 convolution_convert_fusion.3
  40.2 10.6 %fusion = (bf16[2,768,2048]{2,1,0:T(8,128)(2,1)S(1)}, bf16[2,768,2048]{2,1,0:T(8,128)(2,1)}) fusion(bf16[2,768,2048]{2,1,0:T(8,128)(2,1)S(1)} %convolution_convert_fusion.3, bf16[2,768,384]{2,1,0:T(8,128)(2,1)S(1)} %bitcast.227, bf16[2,2,384,2048]{3,2,1,0:T(8,128)(2,1)} %param.14), kind=kOutput, calls=%fused_computation.12 | convolution fusion | flops 2444230656 | bytes 23199744 | tf_op jit(solution)/shard_map/end,edf->enf/dot_general | solution.py:105
  65.9 7.9 %all-to-all-done.2 = bf16[2,768,384]{2,0,1:T(2,128)(2,1)S(1)} async-done(((bf16[2,768,384]{2,0,1:T(2,128)(2,1)}), bf16[2,768,384]{2,0,1:T(2,128)(2,1)S(1)}, u32[]{:S(2)}, u32[]{:S(2)}) %all-to-all-start.2) | async-done | bytes 1179680 | tf_op jit(solution)/shard_map/all_to_all | solution.py:108
  85.3 5.2 all-to-all-done
  96.0 9.8 %all-to-all-done.3 = bf16[8,192,384]{2,1,0:T(8,128)(2,1)} async-done(((bf16[8,192,384]{2,1,0:T(8,128)(2,1)}), bf16[8,192,384]{2,1,0:T(8,128)(2,1)}, u32[]{:S(2)}, u32[]{:S(2)}) %all-to-all-start.3) | async-done | bytes 1179680 | tf_op jit(solution)/shard_map/all_to_all | solution.py:103
  107.4 7.4 %convolution_convert_fusion = bf16[2,768,2048]{2,1,0:T(8,128)(2,1)} fusion(bf16[2,768,384]{2,1,0:T(8,128)(2,1)S(1)} %bitcast.237, bf16[2,2,384,2048]{3,2,1,0:T(8,128)(2,1)} %param.13), kind=kOutput, calls=%fused_computation.34 | convolution fusion | flops 2419064832 | bytes 10616832 | tf_op jit(solution)/shard_map/end,edf->enf/dot_general | solution.py:104
  114.8 5.3 convolution_convert_fusion.1
  120.1 17.2 %fusion.19 = (bf16[2,768,2048]{2,1,0:T(8,128)(2,1)}, bf16[2,768,2048]{2,1,0:T(8,128)(2,1)}, bf16[2,768,2048]{2,1,0:T(8,128)(2,1)}) fusion(bf16[2,768,2048]{2,1,0:T(8,128)(2,1)} %convolution_convert_fusion, bf16[2,768,2048]{2,1,0:T(8,128)(2,1)} %convolution_convert_fusion.1, bf16[2,768,384]{2,1,0:T(8,128)(2,1)S(1)} %bitcast.234, ...), kind=kOutput, calls=%fused_computation.31 | convolution fusion | flops 2472542208 | bytes 35782656 | tf_op jit(solution)/shard_map/end,efd->enf/dot_general | solution.py:126
  137.3 7.3 %convolution_convert_fusion.9.refs_0_ = bf16[2,384,2048]{2,1,0:T(8,128)(2,1)} fusion(bf16[2,768,384]{2,1,0:T(8,128)(2,1)S(1)} %bitcast.239, bf16[2,768,2048]{2,1,0:T(8,128)(2,1)} %get-tuple-element.43), kind=kOutput, calls=%fused_computation.43 | convolution fusion | flops 2417491968 | bytes 10616832 | tf_op jit(solution)/shard_map/end,enf->edf/dot_general | solution.py:134
  153.7 8.0 %pack.2 = bf16[64,576,128]{2,1,0:T(8,128)(2,1)} custom-call(bf16[2,384,2048]{2,1,0:T(8,128)(2,1)} %convolution_convert_fusion.9.refs_0_, bf16[2,384,2048]{2,1,0:T(8,128)(2,1)} %convolution_convert_fusion.8.refs_1_, bf16[2,2048,384]{2,1,0:T(8,128)(2,1)} %convolution_convert_fusion.7.refs_2_), custom_call_target="tpu_custom_call" | custom-call | flops 100000000 | bytes 18874368 | tf_op jit(solution)/shard_map/pack/pallas_call | solution.py:54
  161.7 6.7 fusion.20
  168.4 7.2 %add_convert_fusion.1 = bf16[2,768,384]{2,1,0:T(8,128)(2,1)S(1)} fusion(f32[2,768,384]{2,1,0:T(8,128)S(1)} %fusion.20, bf16[2,768,2048]{2,1,0:T(8,128)(2,1)} %get-tuple-element.42, bf16[2,2,384,2048]{3,2,1,0:T(8,128)(2,1)} %param.14), kind=kOutput, calls=%fused_computation.87 | convolution fusion | flops 2417098752 | bytes 12976128 | tf_op jit(solution)/shard_map/enf,edf->end/dot_general | solution.py:131
  183.1 8.5 %all-to-all-done.4 = bf16[2,768,384]{2,0,1:T(2,128)(2,1)S(1)} async-done(((bf16[2,768,384]{2,0,1:T(2,128)(2,1)}), bf16[2,768,384]{2,0,1:T(2,128)(2,1)S(1)}, u32[]{:S(2)}, u32[]{:S(2)}) %all-to-all-start.4) | async-done | bytes 1179680 | tf_op jit(solution)/shard_map/all_to_all | solution.py:132
  197.5 12.9 %all_to_all.142 = bf16[8,192,384]{2,1,0:T(8,128)(2,1)S(1)} all-to-all(bf16[8,192,384]{2,1,0:T(8,128)(2,1)S(1)} %bitcast.245), channel_id=1, replica_groups=mesh['rep'=8,'ep'=4,'dp'=8] {'ep'}, dimensions={0} | all-to-all | bytes 2359296 | tf_op jit(solution)/shard_map/all_to_all | solution.py:120
  210.5 110.7 %reduce-scatter.7.cloned.1.call-done = bf16[1,576,128]{2,1,0:T(8,128)(2,1)} async-done(((bf16[64,576,128]{2,1,0:T(8,128)(2,1)}), bf16[1,576,128]{2,1,0:T(8,128)(2,1)}) %reduce-scatter.7.cloned.1.call-update) | async-done | bytes 147472
  321.5 7.9 %convolution_convert_fusion.4.refs_2_ = bf16[2,2048,384]{2,1,0:T(8,128)(2,1)} fusion(bf16[2,768,2048]{2,1,0:T(8,128)(2,1)} %copy-done.35, bf16[2,768,384]{2,1,0:T(8,128)(2,1)S(1)} %bitcast.231), kind=kOutput, calls=%fused_computation.38 | convolution fusion | flops 2417491968 | bytes 10616832 | tf_op jit(solution)/shard_map/enf,end->efd/dot_general | solution.py:133
  329.4 12.4 %fusion.3 = (bf16[2,768,2048]{2,1,0:T(8,128)(2,1)S(1)}, bf16[2,768,2048]{2,1,0:T(8,128)(2,1)}) fusion(bf16[2,768,2048]{2,1,0:T(8,128)(2,1)} %get-tuple-element.64, bf16[2,768,2048]{2,1,0:T(8,128)(2,1)} %copy-done.34, bf16[2,768,384]{2,1,0:T(8,128)(2,1)S(1)} %bitcast.232, bf16[2,2,2048,384]{3,2,1,0:T(8,128)(2,1)} %param.15), kind=kOutput, calls=%fused_computation.15 | convolution fusion | flops 2463105024 | bytes 29491200 | tf_op jit(solution)/shard_map/end,efd->enf/dot_general | solution.py:126
  352.1 8.0 %pack.3 = bf16[64,576,128]{2,1,0:T(8,128)(2,1)} custom-call(bf16[2,384,2048]{2,1,0:T(8,128)(2,1)} %convolution_convert_fusion.6.refs_0_, bf16[2,384,2048]{2,1,0:T(8,128)(2,1)} %convolution_convert_fusion.5.refs_1_, bf16[2,2048,384]{2,1,0:T(8,128)(2,1)} %convolution_convert_fusion.4.refs_2_), custom_call_target="tpu_custom_call" | custom-call | flops 100000000 | bytes 18874368 | tf_op jit(solution)/shard_map/pack/pallas_call | solution.py:54
  360.1 51.6 %all-gather.8.cloned.1.call-done = bf16[36864,128]{1,0:T(8,128)(2,1)} async-done(((bf16[576,128]{1,0:T(8,128)(2,1)}), bf16[36864,128]{1,0:T(8,128)(2,1)}) %all-gather.8.cloned.1.call-update) | async-done | bytes 9437200 | tf_op jit(solution)/shard_map/all_gather | solution.py:183
  411.7 7.1 %fusion.66 = bf16[2,768,384]{2,1,0:T(8,128)(2,1)S(1)} fusion(bf16[2,768,2048]{2,1,0:T(8,128)(2,1)} %get-tuple-element.44, bf16[2,2,2048,384]{3,2,1,0:T(8,128)(2,1)} %param.15), kind=kOutput, calls=%fused_computation.96 | convolution fusion | flops 2416508928 | bytes 10616832 | tf_op jit(solution)/shard_map/enf,efd->end/dot_general | solution.py:107
  425.3 6.5 fusion.30
  431.8 7.2 %add_convert_fusion = bf16[2,768,384]{2,1,0:T(8,128)(2,1)S(1)} fusion(f32[2,768,384]{2,1,0:T(8,128)S(1)} %fusion.30, bf16[2,768,2048]{2,1,0:T(8,128)(2,1)} %copy-done.36, bf16[2,2,384,2048]{3,2,1,0:T(8,128)(2,1)} %param.13), kind=kOutput, calls=%fused_computation.86 | convolution fusion | flops 2417098752 | bytes 12976128 | tf_op jit(solution)/shard_map/enf,edf->end/dot_general | solution.py:131
  451.8 10.0 %all-to-all-done.6 = bf16[2,768,384]{2,0,1:T(2,128)(2,1)S(1)} async-done(((bf16[2,768,384]{2,0,1:T(2,128)(2,1)}), bf16[2,768,384]{2,0,1:T(2,128)(2,1)S(1)}, u32[]{:S(2)}, u32[]{:S(2)}) %all-to-all-start.6) | async-done | bytes 1179680 | tf_op jit(solution)/shard_map/all_to_all | solution.py:132
  465.3 98.2 %reduce-scatter.9.cloned.1.call-done = bf16[1,576,128]{2,1,0:T(8,128)(2,1)} async-done(((bf16[64,576,128]{2,1,0:T(8,128)(2,1)}), bf16[1,576,128]{2,1,0:T(8,128)(2,1)}) %reduce-scatter.9.cloned.1.call-update) | async-done | bytes 147472
  563.9 18.9 %all_to_all.143 = bf16[8,96,384]{2,1,0:T(8,128)(2,1)S(1)} all-to-all(bf16[8,96,384]{2,1,0:T(8,128)(2,1)S(1)} %bitcast.225), channel_id=1, replica_groups=mesh['rep'=8,'ep'=4,'dp'=8] {'dp'}, dimensions={0} | all-to-all | bytes 1179648 | tf_op jit(solution)/shard_map/all_to_all | solution.py:151
  588.2 8.4 %unpack_1.1 = (bf16[2,2,384,2048]{3,2,1,0:T(8,128)(2,1)}, bf16[2,2,384,2048]{3,2,1,0:T(8,128)(2,1)}, bf16[2,2,2048,384]{3,2,1,0:T(8,128)(2,1)}) custom-call(bf16[64,576,128]{2,1,0:T(8,128)(2,1)} %bitcast.216), custom_call_target="tpu_custom_call" | custom-call | flops 100000000 | bytes 18874368 | tf_op jit(solution)/shard_map/unpack_1/pallas_call | solution.py:71
  596.6 9.8 %all-gather.3 = bf16[4,12,384]{2,1,0:T(8,128)(2,1)S(1)} all-gather(bf16[1,12,384]{2,1,0:T(8,128)(2,1)S(1)} %bitcast.251), channel_id=3, replica_groups=mesh['rep'=8,'ep'=4,'dp'=8] {'ep'}, dimensions={0}, use_global_device_ids=true | all-gather | bytes 46080 | tf_op jit(solution)/shard_map/all_gather | solution.py:153
  606.4 20.4 %all-gather.4 = bf16[8,12,384]{2,1,0:T(8,128)(2,1)S(1)} all-gather(bf16[1,12,384]{2,1,0:T(8,128)(2,1)S(1)} %bitcast.250), channel_id=1, replica_groups=mesh['rep'=8,'ep'=4,'dp'=8] {'rep'}, dimensions={0}, use_global_device_ids=true | all-gather | bytes 82944 | tf_op jit(solution)/shard_map/all_gather | solution.py:155
  626.8 22.5 %all_gather.29 = bf16[768,384]{1,0:T(8,128)(2,1)S(1)} all-gather(bf16[96,384]{1,0:T(8,128)(2,1)S(1)} %reshape.74), channel_id=1, replica_groups=mesh['rep'=8,'ep'=4,'dp'=8] {'dp'}, dimensions={0}, use_global_device_ids=true | all-gather | bytes 663552 | tf_op jit(solution)/shard_map/all_gather | solution.py:155
  653.9 8.4 %unpack_0.1 = (bf16[2,2,384,2048]{3,2,1,0:T(8,128)(2,1)}, bf16[2,2,384,2048]{3,2,1,0:T(8,128)(2,1)}, bf16[2,2,2048,384]{3,2,1,0:T(8,128)(2,1)}) custom-call(bf16[64,576,128]{2,1,0:T(8,128)(2,1)} %bitcast.215, bf16[2,2,384,2048]{3,2,1,0:T(8,128)(2,1)} %get-tuple-element.30.refs_1_, ...), custom_call_target="tpu_custom_call", output_to_operand_aliasing={{0}: (1, {}), {1}: (2, {}), {2}: (3, {})} | custom-call | flops 100000000 | bytes 18874368 | tf_op jit(solution)/shard_map/unpack_0/pallas_call | solution.py:71
  (170 shorter events, 111.3 us)
Async XLA Ops:
  7.2 4.1 copy-start.20
  7.2 4.1 copy-start.14
  12.4 6.9 %copy-start.29 = (f32[2,384,2]{1,2,0:T(2,128)S(1)}, f32[2,384,2]{1,2,0:T(2,128)}, u32[]{:S(2)}) copy-start(f32[2,384,2]{1,2,0:T(2,128)} %param.11) | copy-start | bytes 18436
  14.3 19.7 %all-to-all-start.1 = ((bf16[8,192,384]{2,1,0:T(8,128)(2,1)}), bf16[8,192,384]{2,1,0:T(8,128)(2,1)S(1)}, u32[]{:S(2)}, u32[]{:S(2)}) async-start(bf16[8,192,384]{2,1,0:T(8,128)(2,1)} %bitcast.233), calls=%async_computation.1 | async-start | bytes 2359296 | tf_op jit(solution)/shard_map/all_to_all | solution.py:103
  19.9 40.5 %copy-start.24 = (f32[384]{0:T(512)}, f32[384]{0:T(512)S(1)}, u32[]{:S(2)}) copy-start(f32[384]{0:T(512)S(1)} %get-tuple-element.67) | copy-start | bytes 4612
  19.9 40.5 %copy-start.26 = (f32[384]{0:T(512)}, f32[384]{0:T(512)S(1)}, u32[]{:S(2)}) copy-start(f32[384]{0:T(512)S(1)} %get-tuple-element.66) | copy-start | bytes 4612
  34.1 6.1 copy-start.8
  34.1 16.7 %slice-start = ((s8[6291456]{0:T(1024)(128)(4,1)}), s8[4194304]{0:T(1024)(128)(4,1)S(1)}, s32[]{:S(2)}) async-start(s8[6291456]{0:T(1024)(128)(4,1)} %bitcast.252), calls=%async_computation.16 | async-start | bytes 8388608
  40.2 10.6 %copy-start.34 = (bf16[2,768,2048]{2,1,0:T(8,128)(2,1)}, bf16[2,768,2048]{2,1,0:T(8,128)(2,1)S(1)}, u32[]{:S(2)}) copy-start(bf16[2,768,2048]{2,1,0:T(8,128)(2,1)S(1)} %convolution_convert_fusion.3) | copy-start | bytes 18874372
  40.2 10.6 %slice-start.1 = ((s8[6291456]{0:T(1024)(128)(4,1)}), s8[2097152]{0:T(1024)(128)(4,1)S(1)}, s32[]{:S(2)}) async-start(s8[6291456]{0:T(1024)(128)(4,1)} %bitcast.252), calls=%async_computation.17 | async-start | bytes 4194304
  56.5 17.2 %all-to-all-start.2 = ((bf16[2,768,384]{2,0,1:T(2,128)(2,1)}), bf16[2,768,384]{2,0,1:T(2,128)(2,1)S(1)}, u32[]{:S(2)}, u32[]{:S(2)}) async-start(bf16[2,768,384]{2,0,1:T(2,128)(2,1)} %copy.102), calls=%async_computation.2 | async-start | bytes 2359296 | tf_op jit(solution)/shard_map/all_to_all | solution.py:108
  73.7 6.2 copy-start.28
  74.7 15.7 %all-to-all-start = ((bf16[8,192,384]{2,1,0:T(8,128)(2,1)}), bf16[8,192,384]{2,1,0:T(8,128)(2,1)S(1)}, u32[]{:S(2)}, u32[]{:S(2)}) async-start(bf16[8,192,384]{2,1,0:T(8,128)(2,1)} %bitcast.230), calls=%async_computation | async-start | bytes 2359296 | tf_op jit(solution)/shard_map/all_to_all | solution.py:120
  90.5 15.3 %all-to-all-start.3 = ((bf16[8,192,384]{2,1,0:T(8,128)(2,1)}), bf16[8,192,384]{2,1,0:T(8,128)(2,1)}, u32[]{:S(2)}, u32[]{:S(2)}) async-start(bf16[8,192,384]{2,1,0:T(8,128)(2,1)} %bitcast.236), calls=%async_computation.3 | async-start | bytes 2359296 | tf_op jit(solution)/shard_map/all_to_all | solution.py:103
  94.8 226.5 %reduce-scatter.7.cloned.1.call-start = ((), (), s32[]{:S(2)}) async-start(), calls=%async_computation.14 | async-start | bytes 9584640
  105.8 9.0 %slice-start.2 = ((s8[6291456]{0:T(1024)(128)(4,1)}), s8[4194304]{0:T(1024)(128)(4,1)S(1)}, s32[]{:S(2)}) async-start(s8[6291456]{0:T(1024)(128)(4,1)} %bitcast.254), calls=%async_computation.18 | async-start | bytes 8388608
  107.3 7.4 %slice-start.3 = ((s8[6291456]{0:T(1024)(128)(4,1)}), s8[2097152]{0:T(1024)(128)(4,1)S(1)}, s32[]{:S(2)}) async-start(s8[6291456]{0:T(1024)(128)(4,1)} %bitcast.254), calls=%async_computation.19 | async-start | bytes 4194304
  114.8 5.3 copy-start.10
  137.3 7.3 %copy-start.38 = (bf16[2,768,2048]{2,1,0:T(8,128)(2,1)S(1)}, bf16[2,768,2048]{2,1,0:T(8,128)(2,1)}, u32[]{:S(2)}) copy-start(bf16[2,768,2048]{2,1,0:T(8,128)(2,1)} %get-tuple-element.42) | copy-start | bytes 18874372
  137.3 11.4 %slice-start.4 = ((s8[6291456]{0:T(1024)(128)(4,1)}), s8[4194304]{0:T(1024)(128)(4,1)S(1)}, s32[]{:S(2)}) async-start(s8[6291456]{0:T(1024)(128)(4,1)} %bitcast.256), calls=%async_computation.20 | async-start | bytes 8388608
  144.6 4.1 slice-start.5
  177.8 13.7 %all-to-all-start.4 = ((bf16[2,768,384]{2,0,1:T(2,128)(2,1)}), bf16[2,768,384]{2,0,1:T(2,128)(2,1)S(1)}, u32[]{:S(2)}, u32[]{:S(2)}) async-start(bf16[2,768,384]{2,0,1:T(2,128)(2,1)} %copy.106), calls=%async_computation.4 | async-start | bytes 2359296 | tf_op jit(solution)/shard_map/all_to_all | solution.py:132
  181.4 230.3 %all-gather.8.cloned.1.call-start = ((), (), s32[]{:S(2)}) async-start(), calls=%async_computation.12 | async-start | bytes 9584640 | tf_op jit(solution)/shard_map/all_gather | solution.py:183
  321.3 242.2 %reduce-scatter.9.cloned.1.call-start = ((), (), s32[]{:S(2)}) async-start(), calls=%async_computation.15 | async-start | bytes 9584640
  329.4 12.4 %copy-start.9 = (bf16[4,2,192,384]{3,2,0,1:T(8,128)(2,1)S(1)}, bf16[4,2,192,384]{3,2,0,1:T(8,128)(2,1)}, u32[]{:S(2)}) copy-start(bf16[4,2,192,384]{3,2,0,1:T(8,128)(2,1)} %copy-done.8) | copy-start | bytes 3538948
  341.8 4.7 copy-start.36
  341.8 6.1 copy-start.37
  421.0 20.2 %all-to-all-start.7 = ((bf16[2,768,384]{2,0,1:T(2,128)(2,1)}), bf16[2,768,384]{2,0,1:T(2,128)(2,1)S(1)}, u32[]{:S(2)}, u32[]{:S(2)}) async-start(bf16[2,768,384]{2,0,1:T(2,128)(2,1)} %copy.117), calls=%async_computation.7 | async-start | bytes 2359296 | tf_op jit(solution)/shard_map/all_to_all | solution.py:108
  442.2 19.5 %all-to-all-start.6 = ((bf16[2,768,384]{2,0,1:T(2,128)(2,1)}), bf16[2,768,384]{2,0,1:T(2,128)(2,1)S(1)}, u32[]{:S(2)}, u32[]{:S(2)}) async-start(bf16[2,768,384]{2,0,1:T(2,128)(2,1)} %copy.113), calls=%async_computation.6 | async-start | bytes 2359296 | tf_op jit(solution)/shard_map/all_to_all | solution.py:132
  446.4 207.5 %all-gather.10.cloned.1.call-start = ((), (), s32[]{:S(2)}) async-start(), calls=%async_computation.13 | async-start | bytes 9584640 | tf_op jit(solution)/shard_map/all_gather | solution.py:189
  462.8 100.7 %copy-start.13 = (bf16[384,384]{0,1:T(8,128)(2,1)S(1)}, bf16[384,384]{0,1:T(8,128)(2,1)}, u32[]{:S(2)}) copy-start(bf16[384,384]{0,1:T(8,128)(2,1)} %convolution_convert_fusion.14) | copy-start | bytes 884740
  583.6 13.0 %all-to-all-start.9 = ((bf16[8,12,384]{2,1,0:T(8,128)(2,1)}), bf16[8,12,384]{2,1,0:T(8,128)(2,1)S(1)}, u32[]{:S(2)}, u32[]{:S(2)}) async-start(bf16[8,12,384]{2,1,0:T(8,128)(2,1)} %reshape.66), calls=%async_computation.9 | async-start | bytes 196608 | tf_op jit(solution)/shard_map/all_to_all | solution.py:151
  (25 other events, 42.9 us)
Sparse Core Ops, SparseCore 0:
  161.9 159.3 reduce-scatter.6
  324.0 87.6 all-gather.7
  415.9 147.5 reduce-scatter.8
  566.1 87.7 all-gather.9
